TPU v7x, 32 devices: a whole 2x2x4 slice. The times are simulated.
32 devices in a mesh: lat: 4 (over y, x), lon: 4 (over z), ens: 2 (over core).
Axes of the slice: x: 2, y: 2, z: 4, core: 2. Of those that a mesh axis runs over, the one named last changes fastest.
Arguments:
- parameters: float32 [2, 128, 32, 512], P(None, 'ens', 'lat', 'lon'), may hold values from -1.2 to 1.2, as said below
- initial_height: float32 [32, 512], P('lat', 'lon'), may hold values from -6 to 6
- initial_speed: float32 [2, 32, 512], P(None, 'lat', 'lon'), may hold values from -4 to 4
- obs_slots: int32 [2, 16, 16, 8], P(None, ('lat', 'lon')), may hold values from -1 to 1023, as said below
- obs_values: float32 [2, 16, 16, 8], P(None, ('lat', 'lon')), may hold values from -6 to 6
- obs_precision: float32 [2, 16, 16, 8], P(None, ('lat', 'lon')), may hold values from 0 to 2, as said below
Outputs:
- calibrated: float32 [2, 128, 32, 512], P(None, 'ens', 'lat', 'lon')
Inputs may be any that keep to these rules, and one draw needn't show every extreme that they name: `obs_slots`: for each iteration and owner, the live slots towards one receiver come first and name distinct cells of the owner's block (local index row * 128 + column); no cell is named twice by one owner in one iteration; in each iteration some receiving block has all 8 slots live from every owner. `obs_precision`: zero exactly where the matching slot of obs_slots (with receiver and owner swapped) is empty, 0.5 or more elsewhere. `parameters`: friction rates lie in 0.02 to 0.2, forcing in -1.2 to 1.2.
All inputs are finite; a program needn't handle non-finite values.
Results may differ from a plain program's by a relative error of at most 0.0003.
Values sent between devices are 32-bit elements; how exact they have to be, the bound alone decides.
A program may use at most 64 MiB of HBM per device.

v0:
```python
import math
import jax
import jax.numpy as jnp
from jax import lax
from jax.sharding import PartitionSpec as P

STEPS = 6
ITERS = 2
depth_step = 0.7
gravity_step = 0.7
coriolis = 0.1


def padded_2(value, sides, width, wrap):
    for axis, dim in sides:
        peers, length = (lax.axis_size(axis), value.shape[dim])
        up = [(i, (i + 1) % peers) for i in range(peers if wrap else peers - 1)]
        down = [(j, i) for i, j in up]
        last = lax.slice_in_dim(value, length - width, length, axis=dim)
        leading = lax.slice_in_dim(value, 0, width, axis=dim)
        before = lax.ppermute(last, axis, up)
        after = lax.ppermute(leading, axis, down)
        value = jnp.concatenate([before, value, after], axis=dim)
    return value


def wall_rows(padded):
    row_count = padded.shape[-2]
    position = lax.axis_index("lat")
    last_block = lax.axis_size("lat") - 1
    row_ids = lax.broadcasted_iota(jnp.int32, (row_count, 1), 0)
    lower_wall = jnp.logical_and(row_ids == 0, position == 0)
    upper_wall = jnp.logical_and(row_ids == row_count - 1, position == last_block)
    keep_rows = jnp.logical_not(jnp.logical_or(lower_wall, upper_wall))
    return padded * keep_rows.astype(padded.dtype)


def advance(height, speeds, friction, forcing):
    east_padded = padded_2(speeds[0], (("lon", 2),), 1, True)
    north_padded = padded_2(speeds[1], (("lat", 1),), 1, False)
    east_diff = east_padded[:, :, 2:] - east_padded[:, :, :-2]
    north_diff = north_padded[:, 2:, :] - north_padded[:, :-2, :]
    height = height - depth_step * (east_diff + north_diff) + forcing
    padded_height = padded_2(height, (("lat", 1), ("lon", 2)), 1, True)
    padded_height = wall_rows(padded_height)
    slope_east = padded_height[:, 1:-1, 2:] - padded_height[:, 1:-1, :-2]
    slope_north = padded_height[:, 2:, 1:-1] - padded_height[:, :-2, 1:-1]
    eastward = (1.0 - friction) * speeds[0] - gravity_step * slope_east + coriolis * speeds[1]
    northward = (1.0 - friction) * speeds[1] - gravity_step * slope_north - coriolis * speeds[0]
    return (height, jnp.stack([eastward, northward]))


def forward(parameters, initial_height, initial_speed):
    members = parameters.shape[1]
    height = jnp.broadcast_to(initial_height, (members,) + initial_height.shape)
    speeds = jnp.broadcast_to(initial_speed[:, None], (2, members) + initial_height.shape)
    for substep in range(STEPS):
        height, speeds = advance(height, speeds, parameters[0], parameters[1])
    return height


def predict(height, cells):
    flattened = height.reshape(height.shape[0], -1)
    wanted = cells.reshape(-1)
    picked = jnp.take(flattened, jnp.clip(wanted, 0, flattened.shape[1] - 1), axis=1)
    picked = jnp.where(wanted[None, :] >= 0, picked, jnp.float32(0.0))
    return picked.T.reshape(cells.shape[0], -1)


def gram_terms(predicted, observed, precision):
    members = predicted.shape[1]
    centre = jnp.mean(predicted, axis=1, keepdims=True)
    spread = predicted - centre
    weighted = spread * precision[:, None]
    misfit = observed[:, None] - predicted
    gram_part = jnp.dot(spread.T, weighted, precision=lax.Precision.HIGHEST) / members
    cross_part = jnp.dot(weighted.T, misfit, precision=lax.Precision.HIGHEST) / math.sqrt(members)
    return (gram_part, cross_part)


def solve_weights(gram_part, cross_part):
    members = gram_part.shape[0]
    system = jnp.eye(members, dtype=jnp.float32) + gram_part
    factor = jnp.linalg.cholesky(system)
    weights = jax.scipy.linalg.cho_solve((factor, True), cross_part) / math.sqrt(members)
    return weights - jnp.mean(weights, axis=0, keepdims=True)


def per_device(parameters, initial_height, initial_speed, obs_slots, obs_values, obs_precision):
    owners = obs_slots.shape[2]
    slot_count = obs_slots.shape[3]
    members_here = parameters.shape[1]
    member_block = lax.axis_index("ens")
    owner_values, owner_precision = (
        lax.all_to_all(obs_values[:, 0], ("lat", "lon"), split_axis=1, concat_axis=1, tiled=True),
        lax.all_to_all(
            obs_precision[:, 0], ("lat", "lon"), split_axis=1, concat_axis=1, tiled=True
        ),
    )
    for iteration in range(ITERS):
        height = forward(parameters, initial_height, initial_speed)
        outgoing = predict(height, obs_slots[iteration, 0])
        received = outgoing
        observed = owner_values[iteration]
        precision = owner_precision[iteration]
        received = received.reshape(owners, slot_count, members_here)
        gathered = lax.all_gather(received, "ens", axis=2, tiled=True)
        members = gathered.shape[2]
        gram_part, cross_part = gram_terms(
            gathered.reshape(-1, members), observed.reshape(-1), precision.reshape(-1)
        )
        gram_part, cross_part = lax.psum((gram_part, cross_part), ("lat", "lon"))
        centred = solve_weights(gram_part, cross_part)
        local_weights = lax.dynamic_slice_in_dim(
            centred, member_block * members_here, members_here, 1
        )
        starting = jnp.zeros(
            (2, members_here, parameters.shape[2] * parameters.shape[3]), jnp.float32
        )
        pieces = lax.all_gather(parameters, "ens", axis=1, tiled=True)
        stacked = pieces.reshape(pieces.shape[0], pieces.shape[1], -1)
        increment = starting + jnp.einsum(
            "pjc,jm->pmc", stacked, local_weights, precision=lax.Precision.HIGHEST
        )
        parameters = parameters + increment.reshape(parameters.shape)
    return parameters


def solution(mesh):
    placed = (
        P(None, "ens", "lat", "lon"),
        P("lat", "lon"),
        P(None, "lat", "lon"),
        P(None, ("lat", "lon"), None, None),
        P(None, ("lat", "lon"), None, None),
        P(None, ("lat", "lon"), None, None),
    )
    return jax.shard_map(
        per_device,
        mesh=mesh,
        in_specs=placed,
        out_specs=P(None, "ens", "lat", "lon"),
        check_vma=False,
    )
```

profile of v0, /device:TPU:0, one launch (start us, length us, event | category | flops | bytes accessed | tf_op | source)
XLA Modules:
  0.0 800.0 jit_solution(9738654765726643208)
XLA Ops:
  9.5 5.5 collective-permute-start.3
  15.3 4.2 collective-permute-start
  19.6 6.5 collective-permute-done
  26.2 4.8 collective-permute-done.1
  42.6 12.8 %collective-permute-done.6 = f32[64,10,1]{2,1,0:T(8,128)S(1)} collective-permute-done((f32[64,10,1]{2,1,0:T(8,128)S(1)}, f32[64,10,1]{2,1,0:T(8,128)S(1)}, u32[]{:S(2)}, u32[]{:S(2)}) %collective-permute-start.6) | collective-permute-done | bytes 2592 | tf_op jit(solution)/shard_map/ppermute | solution.py:21
  55.4 6.8 collective-permute-done.7
  64.6 4.5 collective-permute-start.11
  71.5 10.8 %collective-permute-done.8 = f32[64,8,1]{2,1,0:T(8,128)S(1)} collective-permute-done((f32[64,8,1]{2,1,0:T(8,128)S(1)}, f32[64,8,1]{2,1,0:T(8,128)S(1)}, u32[]{:S(2)}, u32[]{:S(2)}) %collective-permute-start.8) | collective-permute-done | bytes 2080 | tf_op jit(solution)/shard_map/ppermute | solution.py:22
  93.5 12.5 %collective-permute-done.14 = f32[64,10,1]{2,1,0:T(8,128)S(1)} collective-permute-done((f32[64,10,1]{2,1,0:T(8,128)S(1)}, f32[64,10,1]{2,1,0:T(8,128)S(1)}, u32[]{:S(2)}, u32[]{:S(2)}) %collective-permute-start.14) | collective-permute-done | bytes 2592 | tf_op jit(solution)/shard_map/ppermute | solution.py:21
  106.0 5.6 collective-permute-done.15
  114.0 4.5 collective-permute-start.19
  121.7 10.4 %collective-permute-done.16 = f32[64,8,1]{2,1,0:T(8,128)S(1)} collective-permute-done((f32[64,8,1]{2,1,0:T(8,128)S(1)}, f32[64,8,1]{2,1,0:T(8,128)S(1)}, u32[]{:S(2)}, u32[]{:S(2)}) %collective-permute-start.16) | collective-permute-done | bytes 2080 | tf_op jit(solution)/shard_map/ppermute | solution.py:22
  148.4 7.9 collective-permute-done.22
  156.3 5.7 collective-permute-done.23
  168.5 4.5 collective-permute-start.27
  173.1 5.0 collective-permute-done.24
  188.6 12.2 %collective-permute-done.30 = f32[64,10,1]{2,1,0:T(8,128)S(1)} collective-permute-done((f32[64,10,1]{2,1,0:T(8,128)S(1)}, f32[64,10,1]{2,1,0:T(8,128)S(1)}, u32[]{:S(2)}, u32[]{:S(2)}) %collective-permute-start.30) | collective-permute-done | bytes 2592 | tf_op jit(solution)/shard_map/ppermute | solution.py:21
  200.8 6.1 collective-permute-done.31
  211.7 4.5 collective-permute-start.35
  216.2 5.8 collective-permute-done.32
  238.8 7.4 collective-permute-done.38
  246.2 6.6 collective-permute-done.39
  259.1 5.2 collective-permute-start.43
  277.9 104.7 %all-reduce.7.cloned.1.call-done = (f32[128,128]{1,0:T(8,128)}, f32[128,128]{0,1:T(8,128)}) async-done(((f32[128,128]{1,0:T(8,128)}, f32[128,128]{0,1:T(8,128)}), (f32[128,128]{1,0:T(8,128)}, f32[128,128]{0,1:T(8,128)})) %all-reduce.7.cloned.1.call-update) | async-done | bytes 131088 | tf_op jit(solution)/shard_map/psum | solution.py:112
  384.2 11.7 %cholesky.44 = f32[128,128]{1,0:T(8,128)S(1)} custom-call(f32[128,128]{1,0:T(8,128)S(1)} %fusion.151), custom_call_target="Cholesky" | custom-call | tf_op jit(solution)/shard_map/jit(cholesky)/cholesky | solution.py:84
  397.3 9.8 %custom-call.8 = f32[1,128,128]{1,2,0:T(8,128)S(1)} custom-call(f32[1,128,128]{2,1,0:T(8,128)S(1)} %fusion.135), custom_call_target="InvertDiagBlocksLowerTriangular" | custom-call | tf_op jit(solution)/shard_map/jit(_cho_solve)/triangular_solve | solution.py:85
  420.9 12.8 %collective-permute-done.46 = f32[64,10,1]{2,1,0:T(8,128)S(1)} collective-permute-done((f32[64,10,1]{2,1,0:T(8,128)S(1)}, f32[64,10,1]{2,1,0:T(8,128)S(1)}, u32[]{:S(2)}, u32[]{:S(2)}) %collective-permute-start.46) | collective-permute-done | bytes 2592 | tf_op jit(solution)/shard_map/ppermute | solution.py:21
  433.7 5.6 collective-permute-done.47
  441.7 4.8 collective-permute-start.51
  448.8 10.4 %collective-permute-done.48 = f32[64,8,1]{2,1,0:T(8,128)S(1)} collective-permute-done((f32[64,8,1]{2,1,0:T(8,128)S(1)}, f32[64,8,1]{2,1,0:T(8,128)S(1)}, u32[]{:S(2)}, u32[]{:S(2)}) %collective-permute-start.48) | collective-permute-done | bytes 2080 | tf_op jit(solution)/shard_map/ppermute | solution.py:22
  470.8 12.6 %collective-permute-done.54 = f32[64,10,1]{2,1,0:T(8,128)S(1)} collective-permute-done((f32[64,10,1]{2,1,0:T(8,128)S(1)}, f32[64,10,1]{2,1,0:T(8,128)S(1)}, u32[]{:S(2)}, u32[]{:S(2)}) %collective-permute-start.54) | collective-permute-done | bytes 2592 | tf_op jit(solution)/shard_map/ppermute | solution.py:21
  483.3 6.4 collective-permute-done.55
  492.1 4.5 collective-permute-start.59
  499.4 7.2 collective-permute-done.56
  520.5 12.8 %collective-permute-done.62 = f32[64,10,1]{2,1,0:T(8,128)S(1)} collective-permute-done((f32[64,10,1]{2,1,0:T(8,128)S(1)}, f32[64,10,1]{2,1,0:T(8,128)S(1)}, u32[]{:S(2)}, u32[]{:S(2)}) %collective-permute-start.62) | collective-permute-done | bytes 2592 | tf_op jit(solution)/shard_map/ppermute | solution.py:21
  533.2 6.3 collective-permute-done.63
  541.9 4.5 collective-permute-start.67
  549.4 7.2 collective-permute-done.64
  570.5 12.8 %collective-permute-done.70 = f32[64,10,1]{2,1,0:T(8,128)S(1)} collective-permute-done((f32[64,10,1]{2,1,0:T(8,128)S(1)}, f32[64,10,1]{2,1,0:T(8,128)S(1)}, u32[]{:S(2)}, u32[]{:S(2)}) %collective-permute-start.70) | collective-permute-done | bytes 2592 | tf_op jit(solution)/shard_map/ppermute | solution.py:21
  583.3 4.5 collective-permute-done.71
  590.3 4.5 collective-permute-start.75
  597.8 7.4 collective-permute-done.72
  618.9 12.1 %collective-permute-done.78 = f32[64,10,1]{2,1,0:T(8,128)S(1)} collective-permute-done((f32[64,10,1]{2,1,0:T(8,128)S(1)}, f32[64,10,1]{2,1,0:T(8,128)S(1)}, u32[]{:S(2)}, u32[]{:S(2)}) %collective-permute-start.78) | collective-permute-done | bytes 2592 | tf_op jit(solution)/shard_map/ppermute | solution.py:21
  631.0 4.3 collective-permute-done.79
  640.1 4.5 collective-permute-start.83
  657.6 105.3 %all-reduce.5.cloned.1.call-done = (f32[128,128]{1,0:T(8,128)}, f32[128,128]{0,1:T(8,128)}) async-done(((f32[128,128]{1,0:T(8,128)}, f32[128,128]{0,1:T(8,128)}), (f32[128,128]{1,0:T(8,128)}, f32[128,128]{0,1:T(8,128)})) %all-reduce.5.cloned.1.call-update) | async-done | bytes 131088 | tf_op jit(solution)/shard_map/psum | solution.py:112
  764.6 11.7 %cholesky.55 = f32[128,128]{1,0:T(8,128)S(1)} custom-call(f32[128,128]{1,0:T(8,128)S(1)} %fusion.146), custom_call_target="Cholesky" | custom-call | tf_op jit(solution)/shard_map/jit(cholesky)/cholesky | solution.py:84
  777.7 9.8 %custom-call.9 = f32[1,128,128]{1,2,0:T(8,128)S(1)} custom-call(f32[1,128,128]{2,1,0:T(8,128)S(1)} %fusion.136), custom_call_target="InvertDiagBlocksLowerTriangular" | custom-call | tf_op jit(solution)/shard_map/jit(_cho_solve)/triangular_solve | solution.py:85
  (360 shorter events, 225.3 us)
Async XLA Ops:
  8.2 22.9 %collective-permute-start.2 = (f32[64,1,128]{2,1,0:T(1,128)S(1)}, f32[64,1,128]{2,1,0:T(1,128)S(1)}, u32[]{:S(2)}, u32[]{:S(2)}) collective-permute-start(f32[64,1,128]{2,1,0:T(1,128)S(1)} %broadcast_in_dim.82), channel_id=1, source_target_pairs={{8,0},{16,8},{24,16},{9,1},{17,9},{25,17},{10,2},{18,10},{26,18},{... | collective-permute-start | bytes 98312 | tf_op jit(solution)/shard_map/ppermute | solution.py:22
  9.5 21.5 %collective-permute-start.3 = (f32[64,1,128]{2,1,0:T(1,128)S(1)}, f32[64,1,128]{2,1,0:T(1,128)S(1)}, u32[]{:S(2)}, u32[]{:S(2)}) collective-permute-start(f32[64,1,128]{2,1,0:T(1,128)S(1)} %broadcast_in_dim.83), channel_id=1, source_target_pairs={{0,8},{8,16},{16,24},{1,9},{9,17},{17,25},{2,10},{10,18},{18,26},{... | collective-permute-start | bytes 98312 | tf_op jit(solution)/shard_map/ppermute | solution.py:21
  38.7 16.6 %collective-permute-start.6 = (f32[64,10,1]{2,1,0:T(8,128)S(1)}, f32[64,10,1]{2,1,0:T(8,128)S(1)}, u32[]{:S(2)}, u32[]{:S(2)}) collective-permute-start(f32[64,10,1]{2,1,0:T(8,128)S(1)} %get-tuple-element.56), channel_id=1, source_target_pairs={{0,2},{2,4},{4,6},{6,0},{1,3},{3,5},{5,7},{7,1},{8,10},{10,12},{12... | collective-permute-start | bytes 7688 | tf_op jit(solution)/shard_map/ppermute | solution.py:21
  40.4 21.8 %collective-permute-start.7 = (f32[64,10,1]{2,1,0:T(8,128)S(1)}, f32[64,10,1]{2,1,0:T(8,128)S(1)}, u32[]{:S(2)}, u32[]{:S(2)}) collective-permute-start(f32[64,10,1]{2,1,0:T(8,128)S(1)} %get-tuple-element.57), channel_id=1, source_target_pairs={{2,0},{4,2},{6,4},{0,6},{3,1},{5,3},{7,5},{1,7},{10,8},{12,10},{14... | collective-permute-start | bytes 7688 | tf_op jit(solution)/shard_map/ppermute | solution.py:22
  63.3 18.9 %collective-permute-start.10 = (f32[64,1,128]{2,1,0:T(1,128)S(1)}, f32[64,1,128]{2,1,0:T(1,128)S(1)}, u32[]{:S(2)}, u32[]{:S(2)}) collective-permute-start(f32[64,1,128]{2,1,0:T(1,128)S(1)} %get-tuple-element.114), channel_id=1, source_target_pairs={{8,0},{16,8},{24,16},{9,1},{17,9},{25,17},{10,2},{18,10},{26,18},{... | collective-permute-start | bytes 98312 | tf_op jit(solution)/shard_map/ppermute | solution.py:22
  64.6 17.6 %collective-permute-start.11 = (f32[64,1,128]{2,1,0:T(1,128)S(1)}, f32[64,1,128]{2,1,0:T(1,128)S(1)}, u32[]{:S(2)}, u32[]{:S(2)}) collective-permute-start(f32[64,1,128]{2,1,0:T(1,128)S(1)} %get-tuple-element.115), channel_id=1, source_target_pairs={{0,8},{8,16},{16,24},{1,9},{9,17},{17,25},{2,10},{10,18},{18,26},{... | collective-permute-start | bytes 98312 | tf_op jit(solution)/shard_map/ppermute | solution.py:21
  69.3 12.9 %collective-permute-start.8 = (f32[64,8,1]{2,1,0:T(8,128)S(1)}, f32[64,8,1]{2,1,0:T(8,128)S(1)}, u32[]{:S(2)}, u32[]{:S(2)}) collective-permute-start(f32[64,8,1]{2,1,0:T(8,128)S(1)} %get-tuple-element.112), channel_id=1, source_target_pairs={{2,0},{4,2},{6,4},{0,6},{3,1},{5,3},{7,5},{1,7},{10,8},{12,10},{14... | collective-permute-start | bytes 6152 | tf_op jit(solution)/shard_map/ppermute | solution.py:22
  89.7 16.4 %collective-permute-start.14 = (f32[64,10,1]{2,1,0:T(8,128)S(1)}, f32[64,10,1]{2,1,0:T(8,128)S(1)}, u32[]{:S(2)}, u32[]{:S(2)}) collective-permute-start(f32[64,10,1]{2,1,0:T(8,128)S(1)} %get-tuple-element.54), channel_id=1, source_target_pairs={{0,2},{2,4},{4,6},{6,0},{1,3},{3,5},{5,7},{7,1},{8,10},{10,12},{12... | collective-permute-start | bytes 7688 | tf_op jit(solution)/shard_map/ppermute | solution.py:21
  90.0 21.6 %collective-permute-start.15 = (f32[64,10,1]{2,1,0:T(8,128)S(1)}, f32[64,10,1]{2,1,0:T(8,128)S(1)}, u32[]{:S(2)}, u32[]{:S(2)}) collective-permute-start(f32[64,10,1]{2,1,0:T(8,128)S(1)} %get-tuple-element.55), channel_id=1, source_target_pairs={{2,0},{4,2},{6,4},{0,6},{3,1},{5,3},{7,5},{1,7},{10,8},{12,10},{14... | collective-permute-start | bytes 7688 | tf_op jit(solution)/shard_map/ppermute | solution.py:22
  112.7 19.3 %collective-permute-start.18 = (f32[64,1,128]{2,1,0:T(1,128)S(1)}, f32[64,1,128]{2,1,0:T(1,128)S(1)}, u32[]{:S(2)}, u32[]{:S(2)}) collective-permute-start(f32[64,1,128]{2,1,0:T(1,128)S(1)} %get-tuple-element.108), channel_id=1, source_target_pairs={{8,0},{16,8},{24,16},{9,1},{17,9},{25,17},{10,2},{18,10},{26,18},{... | collective-permute-start | bytes 98312 | tf_op jit(solution)/shard_map/ppermute | solution.py:22
  114.0 18.0 %collective-permute-start.19 = (f32[64,1,128]{2,1,0:T(1,128)S(1)}, f32[64,1,128]{2,1,0:T(1,128)S(1)}, u32[]{:S(2)}, u32[]{:S(2)}) collective-permute-start(f32[64,1,128]{2,1,0:T(1,128)S(1)} %get-tuple-element.109), channel_id=1, source_target_pairs={{0,8},{8,16},{16,24},{1,9},{9,17},{17,25},{2,10},{10,18},{18,26},{... | collective-permute-start | bytes 98312 | tf_op jit(solution)/shard_map/ppermute | solution.py:21
  118.7 13.3 %collective-permute-start.16 = (f32[64,8,1]{2,1,0:T(8,128)S(1)}, f32[64,8,1]{2,1,0:T(8,128)S(1)}, u32[]{:S(2)}, u32[]{:S(2)}) collective-permute-start(f32[64,8,1]{2,1,0:T(8,128)S(1)} %get-tuple-element.106), channel_id=1, source_target_pairs={{2,0},{4,2},{6,4},{0,6},{3,1},{5,3},{7,5},{1,7},{10,8},{12,10},{14... | collective-permute-start | bytes 6152 | tf_op jit(solution)/shard_map/ppermute | solution.py:22
  139.8 16.6 %collective-permute-start.22 = (f32[64,10,1]{2,1,0:T(8,128)}, f32[64,10,1]{2,1,0:T(8,128)S(1)}, u32[]{:S(2)}, u32[]{:S(2)}) collective-permute-start(f32[64,10,1]{2,1,0:T(8,128)} %get-tuple-element.52), channel_id=1, source_target_pairs={{0,2},{2,4},{4,6},{6,0},{1,3},{3,5},{5,7},{7,1},{8,10},{10,12},{12... | collective-permute-start | bytes 7688 | tf_op jit(solution)/shard_map/ppermute | solution.py:21
  140.3 21.7 %collective-permute-start.23 = (f32[64,10,1]{2,1,0:T(8,128)}, f32[64,10,1]{2,1,0:T(8,128)}, u32[]{:S(2)}, u32[]{:S(2)}) collective-permute-start(f32[64,10,1]{2,1,0:T(8,128)} %get-tuple-element.53), channel_id=1, source_target_pairs={{2,0},{4,2},{6,4},{0,6},{3,1},{5,3},{7,5},{1,7},{10,8},{12,10},{14... | collective-permute-start | bytes 7688 | tf_op jit(solution)/shard_map/ppermute | solution.py:22
  144.3 89.0 %all-to-all-start.1 = ((f32[2,16,8]{2,0,1:T(2,128)}), f32[2,16,8]{2,0,1:T(2,128)}, u32[]{:S(2)}, u32[]{:S(2)}) async-start(f32[2,16,8]{2,0,1:T(2,128)} %bitcast.16), calls=%async_computation.1 | async-start | bytes 32768 | tf_op jit(solution)/shard_map/all_to_all | solution.py:95
  164.3 13.8 %collective-permute-start.24 = (f32[64,8,1]{2,1,0:T(8,128)S(1)}, f32[64,8,1]{2,1,0:T(8,128)S(1)}, u32[]{:S(2)}, u32[]{:S(2)}) collective-permute-start(f32[64,8,1]{2,1,0:T(8,128)S(1)} %get-tuple-element.100), channel_id=1, source_target_pairs={{2,0},{4,2},{6,4},{0,6},{3,1},{5,3},{7,5},{1,7},{10,8},{12,10},{14... | collective-permute-start | bytes 6152 | tf_op jit(solution)/shard_map/ppermute | solution.py:22
  184.2 16.6 %collective-permute-start.30 = (f32[64,10,1]{2,1,0:T(8,128)S(1)}, f32[64,10,1]{2,1,0:T(8,128)S(1)}, u32[]{:S(2)}, u32[]{:S(2)}) collective-permute-start(f32[64,10,1]{2,1,0:T(8,128)S(1)} %get-tuple-element.50), channel_id=1, source_target_pairs={{0,2},{2,4},{4,6},{6,0},{1,3},{3,5},{5,7},{7,1},{8,10},{10,12},{12... | collective-permute-start | bytes 7688 | tf_op jit(solution)/shard_map/ppermute | solution.py:21
  184.9 22.1 %collective-permute-start.31 = (f32[64,10,1]{2,1,0:T(8,128)S(1)}, f32[64,10,1]{2,1,0:T(8,128)S(1)}, u32[]{:S(2)}, u32[]{:S(2)}) collective-permute-start(f32[64,10,1]{2,1,0:T(8,128)S(1)} %get-tuple-element.51), channel_id=1, source_target_pairs={{2,0},{4,2},{6,4},{0,6},{3,1},{5,3},{7,5},{1,7},{10,8},{12,10},{14... | collective-permute-start | bytes 7688 | tf_op jit(solution)/shard_map/ppermute | solution.py:22
  208.2 13.9 %collective-permute-start.32 = (f32[64,8,1]{2,1,0:T(8,128)S(1)}, f32[64,8,1]{2,1,0:T(8,128)S(1)}, u32[]{:S(2)}, u32[]{:S(2)}) collective-permute-start(f32[64,8,1]{2,1,0:T(8,128)S(1)} %get-tuple-element.94), channel_id=1, source_target_pairs={{2,0},{4,2},{6,4},{0,6},{3,1},{5,3},{7,5},{1,7},{10,8},{12,10},{14... | collective-permute-start | bytes 6152 | tf_op jit(solution)/shard_map/ppermute | solution.py:22
  210.3 11.8 %collective-permute-start.33 = (f32[64,8,1]{2,1,0:T(8,128)S(1)}, f32[64,8,1]{2,1,0:T(8,128)S(1)}, u32[]{:S(2)}, u32[]{:S(2)}) collective-permute-start(f32[64,8,1]{2,1,0:T(8,128)S(1)} %get-tuple-element.95), channel_id=1, source_target_pairs={{0,2},{2,4},{4,6},{6,0},{1,3},{3,5},{5,7},{7,1},{8,10},{10,12},{12... | collective-permute-start | bytes 6152 | tf_op jit(solution)/shard_map/ppermute | solution.py:21
  229.4 16.8 %collective-permute-start.38 = (f32[64,10,1]{2,1,0:T(8,128)}, f32[64,10,1]{2,1,0:T(8,128)S(1)}, u32[]{:S(2)}, u32[]{:S(2)}) collective-permute-start(f32[64,10,1]{2,1,0:T(8,128)} %get-tuple-element.48), channel_id=1, source_target_pairs={{0,2},{2,4},{4,6},{6,0},{1,3},{3,5},{5,7},{7,1},{8,10},{10,12},{12... | collective-permute-start | bytes 7688 | tf_op jit(solution)/shard_map/ppermute | solution.py:21
  230.0 22.8 %collective-permute-start.39 = (f32[64,10,1]{2,1,0:T(8,128)S(1)}, f32[64,10,1]{2,1,0:T(8,128)}, u32[]{:S(2)}, u32[]{:S(2)}) collective-permute-start(f32[64,10,1]{2,1,0:T(8,128)S(1)} %get-tuple-element.49), channel_id=1, source_target_pairs={{2,0},{4,2},{6,4},{0,6},{3,1},{5,3},{7,5},{1,7},{10,8},{12,10},{14... | collective-permute-start | bytes 7688 | tf_op jit(solution)/shard_map/ppermute | solution.py:22
  233.2 31.0 %all-to-all-start = ((f32[2,16,8]{2,0,1:T(2,128)}), f32[2,16,8]{2,0,1:T(2,128)}, u32[]{:S(2)}, u32[]{:S(2)}) async-start(f32[2,16,8]{2,0,1:T(2,128)} %bitcast.208), calls=%async_computation | async-start | bytes 32768 | tf_op jit(solution)/shard_map/all_to_all | solution.py:96
  237.4 145.1 %all-reduce.7.cloned.1.call-start = ((), (), s32[]{:S(2)}) async-start(), calls=%async_computation.5 | async-start | bytes 262144 | tf_op jit(solution)/shard_map/psum | solution.py:112
  255.1 13.8 %collective-permute-start.40 = (f32[64,8,1]{2,1,0:T(8,128)S(1)}, f32[64,8,1]{2,1,0:T(8,128)S(1)}, u32[]{:S(2)}, u32[]{:S(2)}) collective-permute-start(f32[64,8,1]{2,1,0:T(8,128)S(1)} %get-tuple-element.88), channel_id=1, source_target_pairs={{2,0},{4,2},{6,4},{0,6},{3,1},{5,3},{7,5},{1,7},{10,8},{12,10},{14... | collective-permute-start | bytes 6152 | tf_op jit(solution)/shard_map/ppermute | solution.py:22
  257.2 11.7 %collective-permute-start.41 = (f32[64,8,1]{2,1,0:T(8,128)S(1)}, f32[64,8,1]{2,1,0:T(8,128)S(1)}, u32[]{:S(2)}, u32[]{:S(2)}) collective-permute-start(f32[64,8,1]{2,1,0:T(8,128)S(1)} %get-tuple-element.89), channel_id=1, source_target_pairs={{0,2},{2,4},{4,6},{6,0},{1,3},{3,5},{5,7},{7,1},{8,10},{10,12},{12... | collective-permute-start | bytes 6152 | tf_op jit(solution)/shard_map/ppermute | solution.py:21
  277.2 130.5 %all-gather.3.cloned.1.call-start = ((), (), s32[]{:S(2)}) async-start(), calls=%async_computation.2 | async-start | bytes 1572864 | tf_op jit(solution)/shard_map/all_gather | solution.py:120
  277.8 485.1 %all-reduce.5.cloned.1.call-start = ((), (), s32[]{:S(2)}) async-start(), calls=%async_computation.4 | async-start | bytes 262144 | tf_op jit(solution)/shard_map/psum | solution.py:112
  417.1 16.6 %collective-permute-start.46 = (f32[64,10,1]{2,1,0:T(8,128)S(1)}, f32[64,10,1]{2,1,0:T(8,128)S(1)}, u32[]{:S(2)}, u32[]{:S(2)}) collective-permute-start(f32[64,10,1]{2,1,0:T(8,128)S(1)} %get-tuple-element.44), channel_id=1, source_target_pairs={{0,2},{2,4},{4,6},{6,0},{1,3},{3,5},{5,7},{7,1},{8,10},{10,12},{12... | collective-permute-start | bytes 7688 | tf_op jit(solution)/shard_map/ppermute | solution.py:21
  417.9 21.4 %collective-permute-start.47 = (f32[64,10,1]{2,1,0:T(8,128)S(1)}, f32[64,10,1]{2,1,0:T(8,128)S(1)}, u32[]{:S(2)}, u32[]{:S(2)}) collective-permute-start(f32[64,10,1]{2,1,0:T(8,128)S(1)} %get-tuple-element.45), channel_id=1, source_target_pairs={{2,0},{4,2},{6,4},{0,6},{3,1},{5,3},{7,5},{1,7},{10,8},{12,10},{14... | collective-permute-start | bytes 7688 | tf_op jit(solution)/shard_map/ppermute | solution.py:22
  440.4 18.8 %collective-permute-start.50 = (f32[64,1,128]{2,1,0:T(1,128)S(1)}, f32[64,1,128]{2,1,0:T(1,128)S(1)}, u32[]{:S(2)}, u32[]{:S(2)}) collective-permute-start(f32[64,1,128]{2,1,0:T(1,128)S(1)} %get-tuple-element.84), channel_id=1, source_target_pairs={{8,0},{16,8},{24,16},{9,1},{17,9},{25,17},{10,2},{18,10},{26,18},{... | collective-permute-start | bytes 98312 | tf_op jit(solution)/shard_map/ppermute | solution.py:22
  441.7 17.6 %collective-permute-start.51 = (f32[64,1,128]{2,1,0:T(1,128)S(1)}, f32[64,1,128]{2,1,0:T(1,128)S(1)}, u32[]{:S(2)}, u32[]{:S(2)}) collective-permute-start(f32[64,1,128]{2,1,0:T(1,128)S(1)} %get-tuple-element.85), channel_id=1, source_target_pairs={{0,8},{8,16},{16,24},{1,9},{9,17},{17,25},{2,10},{10,18},{18,26},{... | collective-permute-start | bytes 98312 | tf_op jit(solution)/shard_map/ppermute | solution.py:21
  446.6 12.6 %collective-permute-start.48 = (f32[64,8,1]{2,1,0:T(8,128)S(1)}, f32[64,8,1]{2,1,0:T(8,128)S(1)}, u32[]{:S(2)}, u32[]{:S(2)}) collective-permute-start(f32[64,8,1]{2,1,0:T(8,128)S(1)} %get-tuple-element.82), channel_id=1, source_target_pairs={{2,0},{4,2},{6,4},{0,6},{3,1},{5,3},{7,5},{1,7},{10,8},{12,10},{14... | collective-permute-start | bytes 6152 | tf_op jit(solution)/shard_map/ppermute | solution.py:22
  466.7 16.6 %collective-permute-start.54 = (f32[64,10,1]{2,1,0:T(8,128)S(1)}, f32[64,10,1]{2,1,0:T(8,128)S(1)}, u32[]{:S(2)}, u32[]{:S(2)}) collective-permute-start(f32[64,10,1]{2,1,0:T(8,128)S(1)} %get-tuple-element.42), channel_id=1, source_target_pairs={{0,2},{2,4},{4,6},{6,0},{1,3},{3,5},{5,7},{7,1},{8,10},{10,12},{12... | collective-permute-start | bytes 7688 | tf_op jit(solution)/shard_map/ppermute | solution.py:21
  468.1 21.7 %collective-permute-start.55 = (f32[64,10,1]{2,1,0:T(8,128)S(1)}, f32[64,10,1]{2,1,0:T(8,128)S(1)}, u32[]{:S(2)}, u32[]{:S(2)}) collective-permute-start(f32[64,10,1]{2,1,0:T(8,128)S(1)} %get-tuple-element.43), channel_id=1, source_target_pairs={{2,0},{4,2},{6,4},{0,6},{3,1},{5,3},{7,5},{1,7},{10,8},{12,10},{14... | collective-permute-start | bytes 7688 | tf_op jit(solution)/shard_map/ppermute | solution.py:22
  490.8 19.2 %collective-permute-start.58 = (f32[64,1,128]{2,1,0:T(1,128)S(1)}, f32[64,1,128]{2,1,0:T(1,128)S(1)}, u32[]{:S(2)}, u32[]{:S(2)}) collective-permute-start(f32[64,1,128]{2,1,0:T(1,128)S(1)} %get-tuple-element.78), channel_id=1, source_target_pairs={{8,0},{16,8},{24,16},{9,1},{17,9},{25,17},{10,2},{18,10},{26,18},{... | collective-permute-start | bytes 98312 | tf_op jit(solution)/shard_map/ppermute | solution.py:22
  492.1 17.9 %collective-permute-start.59 = (f32[64,1,128]{2,1,0:T(1,128)S(1)}, f32[64,1,128]{2,1,0:T(1,128)S(1)}, u32[]{:S(2)}, u32[]{:S(2)}) collective-permute-start(f32[64,1,128]{2,1,0:T(1,128)S(1)} %get-tuple-element.79), channel_id=1, source_target_pairs={{0,8},{8,16},{16,24},{1,9},{9,17},{17,25},{2,10},{10,18},{18,26},{... | collective-permute-start | bytes 98312 | tf_op jit(solution)/shard_map/ppermute | solution.py:21
  516.6 16.6 %collective-permute-start.62 = (f32[64,10,1]{2,1,0:T(8,128)S(1)}, f32[64,10,1]{2,1,0:T(8,128)S(1)}, u32[]{:S(2)}, u32[]{:S(2)}) collective-permute-start(f32[64,10,1]{2,1,0:T(8,128)S(1)} %get-tuple-element.40), channel_id=1, source_target_pairs={{0,2},{2,4},{4,6},{6,0},{1,3},{3,5},{5,7},{7,1},{8,10},{10,12},{12... | collective-permute-start | bytes 7688 | tf_op jit(solution)/shard_map/ppermute | solution.py:21
  518.1 21.4 %collective-permute-start.63 = (f32[64,10,1]{2,1,0:T(8,128)S(1)}, f32[64,10,1]{2,1,0:T(8,128)S(1)}, u32[]{:S(2)}, u32[]{:S(2)}) collective-permute-start(f32[64,10,1]{2,1,0:T(8,128)S(1)} %get-tuple-element.41), channel_id=1, source_target_pairs={{2,0},{4,2},{6,4},{0,6},{3,1},{5,3},{7,5},{1,7},{10,8},{12,10},{14... | collective-permute-start | bytes 7688 | tf_op jit(solution)/shard_map/ppermute | solution.py:22
  540.6 19.4 %collective-permute-start.66 = (f32[64,1,128]{2,1,0:T(1,128)S(1)}, f32[64,1,128]{2,1,0:T(1,128)S(1)}, u32[]{:S(2)}, u32[]{:S(2)}) collective-permute-start(f32[64,1,128]{2,1,0:T(1,128)S(1)} %get-tuple-element.72), channel_id=1, source_target_pairs={{8,0},{16,8},{24,16},{9,1},{17,9},{25,17},{10,2},{18,10},{26,18},{... | collective-permute-start | bytes 98312 | tf_op jit(solution)/shard_map/ppermute | solution.py:22
  541.9 18.1 %collective-permute-start.67 = (f32[64,1,128]{2,1,0:T(1,128)S(1)}, f32[64,1,128]{2,1,0:T(1,128)S(1)}, u32[]{:S(2)}, u32[]{:S(2)}) collective-permute-start(f32[64,1,128]{2,1,0:T(1,128)S(1)} %get-tuple-element.73), channel_id=1, source_target_pairs={{0,8},{8,16},{16,24},{1,9},{9,17},{17,25},{2,10},{10,18},{18,26},{... | collective-permute-start | bytes 98312 | tf_op jit(solution)/shard_map/ppermute | solution.py:21
  566.7 16.6 %collective-permute-start.70 = (f32[64,10,1]{2,1,0:T(8,128)S(1)}, f32[64,10,1]{2,1,0:T(8,128)S(1)}, u32[]{:S(2)}, u32[]{:S(2)}) collective-permute-start(f32[64,10,1]{2,1,0:T(8,128)S(1)} %get-tuple-element.38), channel_id=1, source_target_pairs={{0,2},{2,4},{4,6},{6,0},{1,3},{3,5},{5,7},{7,1},{8,10},{10,12},{12... | collective-permute-start | bytes 7688 | tf_op jit(solution)/shard_map/ppermute | solution.py:21
  568.2 19.6 %collective-permute-start.71 = (f32[64,10,1]{2,1,0:T(8,128)S(1)}, f32[64,10,1]{2,1,0:T(8,128)S(1)}, u32[]{:S(2)}, u32[]{:S(2)}) collective-permute-start(f32[64,10,1]{2,1,0:T(8,128)S(1)} %get-tuple-element.39), channel_id=1, source_target_pairs={{2,0},{4,2},{6,4},{0,6},{3,1},{5,3},{7,5},{1,7},{10,8},{12,10},{14... | collective-permute-start | bytes 7688 | tf_op jit(solution)/shard_map/ppermute | solution.py:22
  589.0 19.3 %collective-permute-start.74 = (f32[64,1,128]{2,1,0:T(1,128)S(1)}, f32[64,1,128]{2,1,0:T(1,128)S(1)}, u32[]{:S(2)}, u32[]{:S(2)}) collective-permute-start(f32[64,1,128]{2,1,0:T(1,128)S(1)} %get-tuple-element.66), channel_id=1, source_target_pairs={{8,0},{16,8},{24,16},{9,1},{17,9},{25,17},{10,2},{18,10},{26,18},{... | collective-permute-start | bytes 98312 | tf_op jit(solution)/shard_map/ppermute | solution.py:22
  590.3 18.0 %collective-permute-start.75 = (f32[64,1,128]{2,1,0:T(1,128)S(1)}, f32[64,1,128]{2,1,0:T(1,128)S(1)}, u32[]{:S(2)}, u32[]{:S(2)}) collective-permute-start(f32[64,1,128]{2,1,0:T(1,128)S(1)} %get-tuple-element.67), channel_id=1, source_target_pairs={{0,8},{8,16},{16,24},{1,9},{9,17},{17,25},{2,10},{10,18},{18,26},{... | collective-permute-start | bytes 98312 | tf_op jit(solution)/shard_map/ppermute | solution.py:21
  615.0 16.0 %collective-permute-start.78 = (f32[64,10,1]{2,1,0:T(8,128)S(1)}, f32[64,10,1]{2,1,0:T(8,128)S(1)}, u32[]{:S(2)}, u32[]{:S(2)}) collective-permute-start(f32[64,10,1]{2,1,0:T(8,128)S(1)} %get-tuple-element.36), channel_id=1, source_target_pairs={{0,2},{2,4},{4,6},{6,0},{1,3},{3,5},{5,7},{7,1},{8,10},{10,12},{12... | collective-permute-start | bytes 7688 | tf_op jit(solution)/shard_map/ppermute | solution.py:21
  616.6 18.8 %collective-permute-start.79 = (f32[64,10,1]{2,1,0:T(8,128)S(1)}, f32[64,10,1]{2,1,0:T(8,128)S(1)}, u32[]{:S(2)}, u32[]{:S(2)}) collective-permute-start(f32[64,10,1]{2,1,0:T(8,128)S(1)} %get-tuple-element.37), channel_id=1, source_target_pairs={{2,0},{4,2},{6,4},{0,6},{3,1},{5,3},{7,5},{1,7},{10,8},{12,10},{14... | collective-permute-start | bytes 7688 | tf_op jit(solution)/shard_map/ppermute | solution.py:22
  657.0 131.1 %all-gather.5.cloned.1.call-start = ((), (), s32[]{:S(2)}) async-start(), calls=%async_computation.3 | async-start | bytes 1572864 | tf_op jit(solution)/shard_map/all_gather | solution.py:120
  (69 other events, 757.9 us)
Sparse Core Ops, SparseCore 0:
  277.3 105.1 all-reduce.6
  657.2 105.7 all-reduce.4
Sparse Core Ops, SparseCore 1:
  279.2 8.2 all-gather.2
  659.1 8.8 all-gather.4
where the time goes:
time: 810 us; the launch traced here: 800 us
  waiting for transfers between devices  505 us (62%)
  starting transfers between devices  173 us (21%)
  other arithmetic  69.1 us (9%)
  local copies, waits for them, and re-layouts  25.9 us (3%)
  between operations  16.5 us (2%)
    psum x2, waiting for transfers between devices, per_device(): gram_part, cross_part = lax.psum((gram_part, cross_part), ('lat', 'lon'))  210 us
    ppermute x42, waiting for transfers between devices, padded_2(): before = lax.ppermute(last, axis, up)  150 us
    ppermute x42, waiting for transfers between devices, padded_2(): after = lax.ppermute(leading, axis, down)  145 us
    ppermute x42, starting transfers between devices, padded_2(): before = lax.ppermute(last, axis, up)  83.4 us
    ppermute x42, starting transfers between devices, padded_2(): after = lax.ppermute(leading, axis, down)  80.4 us
    another operation x6, other arithmetic, solve_weights(): factor = jnp.linalg.cholesky(system)  24.8 us
    another operation x4, other arithmetic, solve_weights(): jax.scipy.linalg.cho_solve((factor, True), cross_part) / math.sqrt(members)  21 us
  transfers between devices with their start and end apart: 90, of which 57 were waited for; matrix products, arithmetic and copies ran while one was open for 8% of the time, Pallas kernels for 0%

commit v1 on v0

--- a/solution.py
+++ b/solution.py
@@ -109,7 +109,7 @@
         gram_part, cross_part = gram_terms(
             gathered.reshape(-1, members), observed.reshape(-1), precision.reshape(-1)
         )
-        gram_part, cross_part = lax.psum((gram_part, cross_part), ("lat", "lon"))
+        gram_part, cross_part = lax.psum(lax.psum((gram_part, cross_part), "lon"), "lat")
         centred = solve_weights(gram_part, cross_part)
         local_weights = lax.dynamic_slice_in_dim(
             centred, member_block * members_here, members_here, 1

time: 810 us -> 760 us (0.938)
  waiting for transfers between devices: 505 us -> 455 us
    psum x2 -> x4, waiting for transfers between devices: 210 us -> 156 us  [the longest x2 88.4 us: per_device(): lax.psum(lax.psum((gram_part, cross_part), 'lon'), 'lat')]
  transfers between devices with their start and end apart: 90 -> 92, of which waited for: 57 -> 58; matrix products, arithmetic and copies ran while one was open for 8% -> 9% of each run, Pallas kernels for 0% -> 0%
where the time goes in v1:
time: 760 us; the launch traced here: 750 us
  waiting for transfers between devices  455 us (60%)
  starting transfers between devices  172 us (23%)
  other arithmetic  69.2 us (9%)
  local copies, waits for them, and re-layouts  25.9 us (3%)
  between operations  16.2 us (2%)
    ppermute x42, waiting for transfers between devices, padded_2(): after = lax.ppermute(leading, axis, down)  150 us
    ppermute x42, waiting for transfers between devices, padded_2(): before = lax.ppermute(last, axis, up)  148 us
    psum x2, waiting for transfers between devices, per_device(): lax.psum(lax.psum((gram_part, cross_part), 'lon'), 'lat')  88.4 us
    ppermute x42, starting transfers between devices, padded_2(): before = lax.ppermute(last, axis, up)  85.1 us
    ppermute x42, starting transfers between devices, padded_2(): after = lax.ppermute(leading, axis, down)  78.4 us
    psum x2, waiting for transfers between devices, per_device(): lax.psum((gram_part, cross_part), 'lon')  68 us
    another operation x6, other arithmetic, solve_weights(): factor = jnp.linalg.cholesky(system)  24.8 us
    another operation x4, other arithmetic, solve_weights(): jax.scipy.linalg.cho_solve((factor, True), cross_part) / math.sqrt(members)  21 us
  transfers between devices with their start and end apart: 92, of which 58 were waited for; matrix products, arithmetic and copies ran while one was open for 9% of the time, Pallas kernels for 0%

profile of v1, /device:TPU:0, one launch (start us, length us, event | category | flops | bytes accessed | tf_op | source)
XLA Modules:
  0.0 749.6 jit_solution(6522170547363656495)
XLA Ops:
  9.5 5.5 collective-permute-start.3
  19.6 6.5 collective-permute-done
  26.2 4.8 collective-permute-done.1
  42.6 12.8 %collective-permute-done.6 = f32[64,10,1]{2,1,0:T(8,128)S(1)} collective-permute-done((f32[64,10,1]{2,1,0:T(8,128)S(1)}, f32[64,10,1]{2,1,0:T(8,128)S(1)}, u32[]{:S(2)}, u32[]{:S(2)}) %collective-permute-start.6) | collective-permute-done | bytes 2592 | tf_op jit(solution)/shard_map/ppermute | solution.py:21
  55.4 6.8 collective-permute-done.7
  64.6 4.5 collective-permute-start.11
  71.5 10.8 %collective-permute-done.8 = f32[64,8,1]{2,1,0:T(8,128)S(1)} collective-permute-done((f32[64,8,1]{2,1,0:T(8,128)S(1)}, f32[64,8,1]{2,1,0:T(8,128)S(1)}, u32[]{:S(2)}, u32[]{:S(2)}) %collective-permute-start.8) | collective-permute-done | bytes 2080 | tf_op jit(solution)/shard_map/ppermute | solution.py:22
  93.5 12.5 %collective-permute-done.14 = f32[64,10,1]{2,1,0:T(8,128)S(1)} collective-permute-done((f32[64,10,1]{2,1,0:T(8,128)S(1)}, f32[64,10,1]{2,1,0:T(8,128)S(1)}, u32[]{:S(2)}, u32[]{:S(2)}) %collective-permute-start.14) | collective-permute-done | bytes 2592 | tf_op jit(solution)/shard_map/ppermute | solution.py:21
  106.0 5.6 collective-permute-done.15
  114.0 4.5 collective-permute-start.19
  121.7 10.4 %collective-permute-done.16 = f32[64,8,1]{2,1,0:T(8,128)S(1)} collective-permute-done((f32[64,8,1]{2,1,0:T(8,128)S(1)}, f32[64,8,1]{2,1,0:T(8,128)S(1)}, u32[]{:S(2)}, u32[]{:S(2)}) %collective-permute-start.16) | collective-permute-done | bytes 2080 | tf_op jit(solution)/shard_map/ppermute | solution.py:22
  148.4 8.0 %collective-permute-done.22 = f32[64,10,1]{2,1,0:T(8,128)S(1)} collective-permute-done((f32[64,10,1]{2,1,0:T(8,128)}, f32[64,10,1]{2,1,0:T(8,128)S(1)}, u32[]{:S(2)}, u32[]{:S(2)}) %collective-permute-start.22) | collective-permute-done | bytes 2592 | tf_op jit(solution)/shard_map/ppermute | solution.py:21
  156.3 5.7 collective-permute-done.23
  168.5 4.5 collective-permute-start.27
  173.1 5.0 collective-permute-done.24
  188.7 12.2 %collective-permute-done.30 = f32[64,10,1]{2,1,0:T(8,128)S(1)} collective-permute-done((f32[64,10,1]{2,1,0:T(8,128)S(1)}, f32[64,10,1]{2,1,0:T(8,128)S(1)}, u32[]{:S(2)}, u32[]{:S(2)}) %collective-permute-start.30) | collective-permute-done | bytes 2592 | tf_op jit(solution)/shard_map/ppermute | solution.py:21
  200.8 6.1 collective-permute-done.31
  216.2 5.8 collective-permute-done.32
  238.8 7.4 collective-permute-done.38
  246.2 6.6 collective-permute-done.39
  259.1 5.2 collective-permute-start.43
  277.2 34.1 %all-reduce.11.cloned.1.call-done = (f32[128,128]{1,0:T(8,128)}, f32[128,128]{0,1:T(8,128)}) async-done(((f32[128,128]{1,0:T(8,128)}, f32[128,128]{0,1:T(8,128)}), (f32[128,128]{1,0:T(8,128)}, f32[128,128]{0,1:T(8,128)})) %all-reduce.11.cloned.1.call-update) | async-done | bytes 131088 | tf_op jit(solution)/shard_map/psum | solution.py:112
  312.0 44.3 %all-reduce.15.cloned.1.call-done = (f32[128,128]{1,0:T(8,128)}, f32[128,128]{0,1:T(8,128)}) async-done(((f32[128,128]{1,0:T(8,128)}, f32[128,128]{0,1:T(8,128)}), (f32[128,128]{1,0:T(8,128)}, f32[128,128]{0,1:T(8,128)})) %all-reduce.15.cloned.1.call-update) | async-done | bytes 131088 | tf_op jit(solution)/shard_map/psum | solution.py:112
  358.0 11.7 %cholesky.44 = f32[128,128]{1,0:T(8,128)S(1)} custom-call(f32[128,128]{1,0:T(8,128)S(1)} %fusion.151), custom_call_target="Cholesky" | custom-call | tf_op jit(solution)/shard_map/jit(cholesky)/cholesky | solution.py:84
  371.1 9.8 %custom-call.8 = f32[1,128,128]{1,2,0:T(8,128)S(1)} custom-call(f32[1,128,128]{2,1,0:T(8,128)S(1)} %fusion.135), custom_call_target="InvertDiagBlocksLowerTriangular" | custom-call | tf_op jit(solution)/shard_map/jit(_cho_solve)/triangular_solve | solution.py:85
  394.7 12.8 %collective-permute-done.46 = f32[64,10,1]{2,1,0:T(8,128)S(1)} collective-permute-done((f32[64,10,1]{2,1,0:T(8,128)S(1)}, f32[64,10,1]{2,1,0:T(8,128)S(1)}, u32[]{:S(2)}, u32[]{:S(2)}) %collective-permute-start.46) | collective-permute-done | bytes 2592 | tf_op jit(solution)/shard_map/ppermute | solution.py:21
  407.5 7.6 %collective-permute-done.47 = f32[64,10,1]{2,1,0:T(8,128)S(1)} collective-permute-done((f32[64,10,1]{2,1,0:T(8,128)S(1)}, f32[64,10,1]{2,1,0:T(8,128)S(1)}, u32[]{:S(2)}, u32[]{:S(2)}) %collective-permute-start.47) | collective-permute-done | bytes 2592 | tf_op jit(solution)/shard_map/ppermute | solution.py:22
  417.5 4.8 collective-permute-start.51
  424.7 7.4 collective-permute-done.48
  447.3 12.6 %collective-permute-done.54 = f32[64,10,1]{2,1,0:T(8,128)S(1)} collective-permute-done((f32[64,10,1]{2,1,0:T(8,128)S(1)}, f32[64,10,1]{2,1,0:T(8,128)S(1)}, u32[]{:S(2)}, u32[]{:S(2)}) %collective-permute-start.54) | collective-permute-done | bytes 2592 | tf_op jit(solution)/shard_map/ppermute | solution.py:21
  459.9 6.5 collective-permute-done.55
  468.8 4.5 collective-permute-start.59
  476.0 7.2 collective-permute-done.56
  497.2 12.8 %collective-permute-done.62 = f32[64,10,1]{2,1,0:T(8,128)S(1)} collective-permute-done((f32[64,10,1]{2,1,0:T(8,128)S(1)}, f32[64,10,1]{2,1,0:T(8,128)S(1)}, u32[]{:S(2)}, u32[]{:S(2)}) %collective-permute-start.62) | collective-permute-done | bytes 2592 | tf_op jit(solution)/shard_map/ppermute | solution.py:21
  510.0 4.9 collective-permute-done.63
  517.4 4.5 collective-permute-start.67
  525.4 7.2 collective-permute-done.64
  546.8 12.8 %collective-permute-done.70 = f32[64,10,1]{2,1,0:T(8,128)S(1)} collective-permute-done((f32[64,10,1]{2,1,0:T(8,128)S(1)}, f32[64,10,1]{2,1,0:T(8,128)S(1)}, u32[]{:S(2)}, u32[]{:S(2)}) %collective-permute-start.70) | collective-permute-done | bytes 2592 | tf_op jit(solution)/shard_map/ppermute | solution.py:21
  566.6 4.5 collective-permute-start.75
  573.3 9.5 %collective-permute-done.72 = f32[64,8,1]{2,1,0:T(8,128)S(1)} collective-permute-done((f32[64,8,1]{2,1,0:T(8,128)S(1)}, f32[64,8,1]{2,1,0:T(8,128)S(1)}, u32[]{:S(2)}, u32[]{:S(2)}) %collective-permute-start.72) | collective-permute-done | bytes 2080 | tf_op jit(solution)/shard_map/ppermute | solution.py:22
  593.8 12.6 %collective-permute-done.78 = f32[64,10,1]{2,1,0:T(8,128)S(1)} collective-permute-done((f32[64,10,1]{2,1,0:T(8,128)S(1)}, f32[64,10,1]{2,1,0:T(8,128)S(1)}, u32[]{:S(2)}, u32[]{:S(2)}) %collective-permute-start.78) | collective-permute-done | bytes 2592 | tf_op jit(solution)/shard_map/ppermute | solution.py:21
  606.4 5.4 collective-permute-done.79
  616.4 4.5 collective-permute-start.83
  621.3 5.5 collective-permute-done.80
  634.2 33.8 %all-reduce.9.cloned.1.call-done = (f32[128,128]{1,0:T(8,128)}, f32[128,128]{0,1:T(8,128)}) async-done(((f32[128,128]{1,0:T(8,128)}, f32[128,128]{0,1:T(8,128)}), (f32[128,128]{1,0:T(8,128)}, f32[128,128]{0,1:T(8,128)})) %all-reduce.9.cloned.1.call-update) | async-done | bytes 131088 | tf_op jit(solution)/shard_map/psum | solution.py:112
  668.7 44.2 %all-reduce.13.cloned.1.call-done = (f32[128,128]{1,0:T(8,128)}, f32[128,128]{0,1:T(8,128)}) async-done(((f32[128,128]{1,0:T(8,128)}, f32[128,128]{0,1:T(8,128)}), (f32[128,128]{1,0:T(8,128)}, f32[128,128]{0,1:T(8,128)})) %all-reduce.13.cloned.1.call-update) | async-done | bytes 131088 | tf_op jit(solution)/shard_map/psum | solution.py:112
  714.6 11.7 %cholesky.55 = f32[128,128]{1,0:T(8,128)S(1)} custom-call(f32[128,128]{1,0:T(8,128)S(1)} %fusion.146), custom_call_target="Cholesky" | custom-call | tf_op jit(solution)/shard_map/jit(cholesky)/cholesky | solution.py:84
  727.6 9.8 %custom-call.9 = f32[1,128,128]{1,2,0:T(8,128)S(1)} custom-call(f32[1,128,128]{2,1,0:T(8,128)S(1)} %fusion.136), custom_call_target="InvertDiagBlocksLowerTriangular" | custom-call | tf_op jit(solution)/shard_map/jit(_cho_solve)/triangular_solve | solution.py:85
  (366 shorter events, 235.1 us)
Async XLA Ops:
  8.2 22.9 %collective-permute-start.2 = (f32[64,1,128]{2,1,0:T(1,128)S(1)}, f32[64,1,128]{2,1,0:T(1,128)S(1)}, u32[]{:S(2)}, u32[]{:S(2)}) collective-permute-start(f32[64,1,128]{2,1,0:T(1,128)S(1)} %broadcast_in_dim.82), channel_id=1, source_target_pairs={{8,0},{16,8},{24,16},{9,1},{17,9},{25,17},{10,2},{18,10},{26,18},{... | collective-permute-start | bytes 98312 | tf_op jit(solution)/shard_map/ppermute | solution.py:22
  9.5 21.5 %collective-permute-start.3 = (f32[64,1,128]{2,1,0:T(1,128)S(1)}, f32[64,1,128]{2,1,0:T(1,128)S(1)}, u32[]{:S(2)}, u32[]{:S(2)}) collective-permute-start(f32[64,1,128]{2,1,0:T(1,128)S(1)} %broadcast_in_dim.83), channel_id=1, source_target_pairs={{0,8},{8,16},{16,24},{1,9},{9,17},{17,25},{2,10},{10,18},{18,26},{... | collective-permute-start | bytes 98312 | tf_op jit(solution)/shard_map/ppermute | solution.py:21
  38.7 16.6 %collective-permute-start.6 = (f32[64,10,1]{2,1,0:T(8,128)S(1)}, f32[64,10,1]{2,1,0:T(8,128)S(1)}, u32[]{:S(2)}, u32[]{:S(2)}) collective-permute-start(f32[64,10,1]{2,1,0:T(8,128)S(1)} %get-tuple-element.60), channel_id=1, source_target_pairs={{0,2},{2,4},{4,6},{6,0},{1,3},{3,5},{5,7},{7,1},{8,10},{10,12},{12... | collective-permute-start | bytes 7688 | tf_op jit(solution)/shard_map/ppermute | solution.py:21
  40.4 21.8 %collective-permute-start.7 = (f32[64,10,1]{2,1,0:T(8,128)S(1)}, f32[64,10,1]{2,1,0:T(8,128)S(1)}, u32[]{:S(2)}, u32[]{:S(2)}) collective-permute-start(f32[64,10,1]{2,1,0:T(8,128)S(1)} %get-tuple-element.61), channel_id=1, source_target_pairs={{2,0},{4,2},{6,4},{0,6},{3,1},{5,3},{7,5},{1,7},{10,8},{12,10},{14... | collective-permute-start | bytes 7688 | tf_op jit(solution)/shard_map/ppermute | solution.py:22
  63.3 18.9 %collective-permute-start.10 = (f32[64,1,128]{2,1,0:T(1,128)S(1)}, f32[64,1,128]{2,1,0:T(1,128)S(1)}, u32[]{:S(2)}, u32[]{:S(2)}) collective-permute-start(f32[64,1,128]{2,1,0:T(1,128)S(1)} %get-tuple-element.118), channel_id=1, source_target_pairs={{8,0},{16,8},{24,16},{9,1},{17,9},{25,17},{10,2},{18,10},{26,18},{... | collective-permute-start | bytes 98312 | tf_op jit(solution)/shard_map/ppermute | solution.py:22
  64.6 17.6 %collective-permute-start.11 = (f32[64,1,128]{2,1,0:T(1,128)S(1)}, f32[64,1,128]{2,1,0:T(1,128)S(1)}, u32[]{:S(2)}, u32[]{:S(2)}) collective-permute-start(f32[64,1,128]{2,1,0:T(1,128)S(1)} %get-tuple-element.119), channel_id=1, source_target_pairs={{0,8},{8,16},{16,24},{1,9},{9,17},{17,25},{2,10},{10,18},{18,26},{... | collective-permute-start | bytes 98312 | tf_op jit(solution)/shard_map/ppermute | solution.py:21
  69.3 12.9 %collective-permute-start.8 = (f32[64,8,1]{2,1,0:T(8,128)S(1)}, f32[64,8,1]{2,1,0:T(8,128)S(1)}, u32[]{:S(2)}, u32[]{:S(2)}) collective-permute-start(f32[64,8,1]{2,1,0:T(8,128)S(1)} %get-tuple-element.116), channel_id=1, source_target_pairs={{2,0},{4,2},{6,4},{0,6},{3,1},{5,3},{7,5},{1,7},{10,8},{12,10},{14... | collective-permute-start | bytes 6152 | tf_op jit(solution)/shard_map/ppermute | solution.py:22
  89.7 16.4 %collective-permute-start.14 = (f32[64,10,1]{2,1,0:T(8,128)S(1)}, f32[64,10,1]{2,1,0:T(8,128)S(1)}, u32[]{:S(2)}, u32[]{:S(2)}) collective-permute-start(f32[64,10,1]{2,1,0:T(8,128)S(1)} %get-tuple-element.58), channel_id=1, source_target_pairs={{0,2},{2,4},{4,6},{6,0},{1,3},{3,5},{5,7},{7,1},{8,10},{10,12},{12... | collective-permute-start | bytes 7688 | tf_op jit(solution)/shard_map/ppermute | solution.py:21
  90.0 21.6 %collective-permute-start.15 = (f32[64,10,1]{2,1,0:T(8,128)S(1)}, f32[64,10,1]{2,1,0:T(8,128)S(1)}, u32[]{:S(2)}, u32[]{:S(2)}) collective-permute-start(f32[64,10,1]{2,1,0:T(8,128)S(1)} %get-tuple-element.59), channel_id=1, source_target_pairs={{2,0},{4,2},{6,4},{0,6},{3,1},{5,3},{7,5},{1,7},{10,8},{12,10},{14... | collective-permute-start | bytes 7688 | tf_op jit(solution)/shard_map/ppermute | solution.py:22
  112.7 19.3 %collective-permute-start.18 = (f32[64,1,128]{2,1,0:T(1,128)S(1)}, f32[64,1,128]{2,1,0:T(1,128)S(1)}, u32[]{:S(2)}, u32[]{:S(2)}) collective-permute-start(f32[64,1,128]{2,1,0:T(1,128)S(1)} %get-tuple-element.112), channel_id=1, source_target_pairs={{8,0},{16,8},{24,16},{9,1},{17,9},{25,17},{10,2},{18,10},{26,18},{... | collective-permute-start | bytes 98312 | tf_op jit(solution)/shard_map/ppermute | solution.py:22
  114.0 18.0 %collective-permute-start.19 = (f32[64,1,128]{2,1,0:T(1,128)S(1)}, f32[64,1,128]{2,1,0:T(1,128)S(1)}, u32[]{:S(2)}, u32[]{:S(2)}) collective-permute-start(f32[64,1,128]{2,1,0:T(1,128)S(1)} %get-tuple-element.113), channel_id=1, source_target_pairs={{0,8},{8,16},{16,24},{1,9},{9,17},{17,25},{2,10},{10,18},{18,26},{... | collective-permute-start | bytes 98312 | tf_op jit(solution)/shard_map/ppermute | solution.py:21
  118.7 13.3 %collective-permute-start.16 = (f32[64,8,1]{2,1,0:T(8,128)S(1)}, f32[64,8,1]{2,1,0:T(8,128)S(1)}, u32[]{:S(2)}, u32[]{:S(2)}) collective-permute-start(f32[64,8,1]{2,1,0:T(8,128)S(1)} %get-tuple-element.110), channel_id=1, source_target_pairs={{2,0},{4,2},{6,4},{0,6},{3,1},{5,3},{7,5},{1,7},{10,8},{12,10},{14... | collective-permute-start | bytes 6152 | tf_op jit(solution)/shard_map/ppermute | solution.py:22
  139.8 16.6 %collective-permute-start.22 = (f32[64,10,1]{2,1,0:T(8,128)}, f32[64,10,1]{2,1,0:T(8,128)S(1)}, u32[]{:S(2)}, u32[]{:S(2)}) collective-permute-start(f32[64,10,1]{2,1,0:T(8,128)} %get-tuple-element.56), channel_id=1, source_target_pairs={{0,2},{2,4},{4,6},{6,0},{1,3},{3,5},{5,7},{7,1},{8,10},{10,12},{12... | collective-permute-start | bytes 7688 | tf_op jit(solution)/shard_map/ppermute | solution.py:21
  140.3 21.7 %collective-permute-start.23 = (f32[64,10,1]{2,1,0:T(8,128)}, f32[64,10,1]{2,1,0:T(8,128)}, u32[]{:S(2)}, u32[]{:S(2)}) collective-permute-start(f32[64,10,1]{2,1,0:T(8,128)} %get-tuple-element.57), channel_id=1, source_target_pairs={{2,0},{4,2},{6,4},{0,6},{3,1},{5,3},{7,5},{1,7},{10,8},{12,10},{14... | collective-permute-start | bytes 7688 | tf_op jit(solution)/shard_map/ppermute | solution.py:22
  144.3 89.0 %all-to-all-start.1 = ((f32[2,16,8]{2,0,1:T(2,128)}), f32[2,16,8]{2,0,1:T(2,128)}, u32[]{:S(2)}, u32[]{:S(2)}) async-start(f32[2,16,8]{2,0,1:T(2,128)} %bitcast.16), calls=%async_computation.1 | async-start | bytes 32768 | tf_op jit(solution)/shard_map/all_to_all | solution.py:95
  164.3 13.8 %collective-permute-start.24 = (f32[64,8,1]{2,1,0:T(8,128)S(1)}, f32[64,8,1]{2,1,0:T(8,128)S(1)}, u32[]{:S(2)}, u32[]{:S(2)}) collective-permute-start(f32[64,8,1]{2,1,0:T(8,128)S(1)} %get-tuple-element.104), channel_id=1, source_target_pairs={{2,0},{4,2},{6,4},{0,6},{3,1},{5,3},{7,5},{1,7},{10,8},{12,10},{14... | collective-permute-start | bytes 6152 | tf_op jit(solution)/shard_map/ppermute | solution.py:22
  184.2 16.6 %collective-permute-start.30 = (f32[64,10,1]{2,1,0:T(8,128)S(1)}, f32[64,10,1]{2,1,0:T(8,128)S(1)}, u32[]{:S(2)}, u32[]{:S(2)}) collective-permute-start(f32[64,10,1]{2,1,0:T(8,128)S(1)} %get-tuple-element.54), channel_id=1, source_target_pairs={{0,2},{2,4},{4,6},{6,0},{1,3},{3,5},{5,7},{7,1},{8,10},{10,12},{12... | collective-permute-start | bytes 7688 | tf_op jit(solution)/shard_map/ppermute | solution.py:21
  184.9 22.1 %collective-permute-start.31 = (f32[64,10,1]{2,1,0:T(8,128)S(1)}, f32[64,10,1]{2,1,0:T(8,128)S(1)}, u32[]{:S(2)}, u32[]{:S(2)}) collective-permute-start(f32[64,10,1]{2,1,0:T(8,128)S(1)} %get-tuple-element.55), channel_id=1, source_target_pairs={{2,0},{4,2},{6,4},{0,6},{3,1},{5,3},{7,5},{1,7},{10,8},{12,10},{14... | collective-permute-start | bytes 7688 | tf_op jit(solution)/shard_map/ppermute | solution.py:22
  208.2 13.9 %collective-permute-start.32 = (f32[64,8,1]{2,1,0:T(8,128)S(1)}, f32[64,8,1]{2,1,0:T(8,128)S(1)}, u32[]{:S(2)}, u32[]{:S(2)}) collective-permute-start(f32[64,8,1]{2,1,0:T(8,128)S(1)} %get-tuple-element.98), channel_id=1, source_target_pairs={{2,0},{4,2},{6,4},{0,6},{3,1},{5,3},{7,5},{1,7},{10,8},{12,10},{14... | collective-permute-start | bytes 6152 | tf_op jit(solution)/shard_map/ppermute | solution.py:22
  229.4 16.8 %collective-permute-start.38 = (f32[64,10,1]{2,1,0:T(8,128)}, f32[64,10,1]{2,1,0:T(8,128)S(1)}, u32[]{:S(2)}, u32[]{:S(2)}) collective-permute-start(f32[64,10,1]{2,1,0:T(8,128)} %get-tuple-element.52), channel_id=1, source_target_pairs={{0,2},{2,4},{4,6},{6,0},{1,3},{3,5},{5,7},{7,1},{8,10},{10,12},{12... | collective-permute-start | bytes 7688 | tf_op jit(solution)/shard_map/ppermute | solution.py:21
  230.0 22.8 %collective-permute-start.39 = (f32[64,10,1]{2,1,0:T(8,128)S(1)}, f32[64,10,1]{2,1,0:T(8,128)}, u32[]{:S(2)}, u32[]{:S(2)}) collective-permute-start(f32[64,10,1]{2,1,0:T(8,128)S(1)} %get-tuple-element.53), channel_id=1, source_target_pairs={{2,0},{4,2},{6,4},{0,6},{3,1},{5,3},{7,5},{1,7},{10,8},{12,10},{14... | collective-permute-start | bytes 7688 | tf_op jit(solution)/shard_map/ppermute | solution.py:22
  233.2 31.0 %all-to-all-start = ((f32[2,16,8]{2,0,1:T(2,128)}), f32[2,16,8]{2,0,1:T(2,128)}, u32[]{:S(2)}, u32[]{:S(2)}) async-start(f32[2,16,8]{2,0,1:T(2,128)} %bitcast.208), calls=%async_computation | async-start | bytes 32768 | tf_op jit(solution)/shard_map/all_to_all | solution.py:96
  237.3 74.1 %all-reduce.11.cloned.1.call-start = ((), (), s32[]{:S(2)}) async-start(), calls=%async_computation.5 | async-start | bytes 262144 | tf_op jit(solution)/shard_map/psum | solution.py:112
  255.0 13.8 %collective-permute-start.40 = (f32[64,8,1]{2,1,0:T(8,128)S(1)}, f32[64,8,1]{2,1,0:T(8,128)S(1)}, u32[]{:S(2)}, u32[]{:S(2)}) collective-permute-start(f32[64,8,1]{2,1,0:T(8,128)S(1)} %get-tuple-element.92), channel_id=1, source_target_pairs={{2,0},{4,2},{6,4},{0,6},{3,1},{5,3},{7,5},{1,7},{10,8},{12,10},{14... | collective-permute-start | bytes 6152 | tf_op jit(solution)/shard_map/ppermute | solution.py:22
  277.2 79.1 %all-reduce.15.cloned.1.call-start = ((), (), s32[]{:S(2)}) async-start(), calls=%async_computation.7 | async-start | bytes 262144 | tf_op jit(solution)/shard_map/psum | solution.py:112
  311.4 70.1 %all-gather.3.cloned.1.call-start = ((), (), s32[]{:S(2)}) async-start(), calls=%async_computation.2 | async-start | bytes 1572864 | tf_op jit(solution)/shard_map/all_gather | solution.py:120
  312.0 356.1 %all-reduce.9.cloned.1.call-start = ((), (), s32[]{:S(2)}) async-start(), calls=%async_computation.4 | async-start | bytes 262144 | tf_op jit(solution)/shard_map/psum | solution.py:112
  390.8 16.7 %collective-permute-start.46 = (f32[64,10,1]{2,1,0:T(8,128)S(1)}, f32[64,10,1]{2,1,0:T(8,128)S(1)}, u32[]{:S(2)}, u32[]{:S(2)}) collective-permute-start(f32[64,10,1]{2,1,0:T(8,128)S(1)} %get-tuple-element.48), channel_id=1, source_target_pairs={{0,2},{2,4},{4,6},{6,0},{1,3},{3,5},{5,7},{7,1},{8,10},{10,12},{12... | collective-permute-start | bytes 7688 | tf_op jit(solution)/shard_map/ppermute | solution.py:21
  392.4 22.7 %collective-permute-start.47 = (f32[64,10,1]{2,1,0:T(8,128)S(1)}, f32[64,10,1]{2,1,0:T(8,128)S(1)}, u32[]{:S(2)}, u32[]{:S(2)}) collective-permute-start(f32[64,10,1]{2,1,0:T(8,128)S(1)} %get-tuple-element.49), channel_id=1, source_target_pairs={{2,0},{4,2},{6,4},{0,6},{3,1},{5,3},{7,5},{1,7},{10,8},{12,10},{14... | collective-permute-start | bytes 7688 | tf_op jit(solution)/shard_map/ppermute | solution.py:22
  416.2 19.6 %collective-permute-start.50 = (f32[64,1,128]{2,1,0:T(1,128)S(1)}, f32[64,1,128]{2,1,0:T(1,128)S(1)}, u32[]{:S(2)}, u32[]{:S(2)}) collective-permute-start(f32[64,1,128]{2,1,0:T(1,128)S(1)} %get-tuple-element.88), channel_id=1, source_target_pairs={{8,0},{16,8},{24,16},{9,1},{17,9},{25,17},{10,2},{18,10},{26,18},{... | collective-permute-start | bytes 98312 | tf_op jit(solution)/shard_map/ppermute | solution.py:22
  417.5 18.3 %collective-permute-start.51 = (f32[64,1,128]{2,1,0:T(1,128)S(1)}, f32[64,1,128]{2,1,0:T(1,128)S(1)}, u32[]{:S(2)}, u32[]{:S(2)}) collective-permute-start(f32[64,1,128]{2,1,0:T(1,128)S(1)} %get-tuple-element.89), channel_id=1, source_target_pairs={{0,8},{8,16},{16,24},{1,9},{9,17},{17,25},{2,10},{10,18},{18,26},{... | collective-permute-start | bytes 98312 | tf_op jit(solution)/shard_map/ppermute | solution.py:21
  443.3 16.6 %collective-permute-start.54 = (f32[64,10,1]{2,1,0:T(8,128)S(1)}, f32[64,10,1]{2,1,0:T(8,128)S(1)}, u32[]{:S(2)}, u32[]{:S(2)}) collective-permute-start(f32[64,10,1]{2,1,0:T(8,128)S(1)} %get-tuple-element.46), channel_id=1, source_target_pairs={{0,2},{2,4},{4,6},{6,0},{1,3},{3,5},{5,7},{7,1},{8,10},{10,12},{12... | collective-permute-start | bytes 7688 | tf_op jit(solution)/shard_map/ppermute | solution.py:21
  444.8 21.6 %collective-permute-start.55 = (f32[64,10,1]{2,1,0:T(8,128)S(1)}, f32[64,10,1]{2,1,0:T(8,128)S(1)}, u32[]{:S(2)}, u32[]{:S(2)}) collective-permute-start(f32[64,10,1]{2,1,0:T(8,128)S(1)} %get-tuple-element.47), channel_id=1, source_target_pairs={{2,0},{4,2},{6,4},{0,6},{3,1},{5,3},{7,5},{1,7},{10,8},{12,10},{14... | collective-permute-start | bytes 7688 | tf_op jit(solution)/shard_map/ppermute | solution.py:22
  467.5 19.0 %collective-permute-start.58 = (f32[64,1,128]{2,1,0:T(1,128)S(1)}, f32[64,1,128]{2,1,0:T(1,128)S(1)}, u32[]{:S(2)}, u32[]{:S(2)}) collective-permute-start(f32[64,1,128]{2,1,0:T(1,128)S(1)} %get-tuple-element.82), channel_id=1, source_target_pairs={{8,0},{16,8},{24,16},{9,1},{17,9},{25,17},{10,2},{18,10},{26,18},{... | collective-permute-start | bytes 98312 | tf_op jit(solution)/shard_map/ppermute | solution.py:22
  468.8 17.8 %collective-permute-start.59 = (f32[64,1,128]{2,1,0:T(1,128)S(1)}, f32[64,1,128]{2,1,0:T(1,128)S(1)}, u32[]{:S(2)}, u32[]{:S(2)}) collective-permute-start(f32[64,1,128]{2,1,0:T(1,128)S(1)} %get-tuple-element.83), channel_id=1, source_target_pairs={{0,8},{8,16},{16,24},{1,9},{9,17},{17,25},{2,10},{10,18},{18,26},{... | collective-permute-start | bytes 98312 | tf_op jit(solution)/shard_map/ppermute | solution.py:21
  493.4 16.6 %collective-permute-start.62 = (f32[64,10,1]{2,1,0:T(8,128)S(1)}, f32[64,10,1]{2,1,0:T(8,128)S(1)}, u32[]{:S(2)}, u32[]{:S(2)}) collective-permute-start(f32[64,10,1]{2,1,0:T(8,128)S(1)} %get-tuple-element.44), channel_id=1, source_target_pairs={{0,2},{2,4},{4,6},{6,0},{1,3},{3,5},{5,7},{7,1},{8,10},{10,12},{12... | collective-permute-start | bytes 7688 | tf_op jit(solution)/shard_map/ppermute | solution.py:21
  494.9 20.0 %collective-permute-start.63 = (f32[64,10,1]{2,1,0:T(8,128)S(1)}, f32[64,10,1]{2,1,0:T(8,128)S(1)}, u32[]{:S(2)}, u32[]{:S(2)}) collective-permute-start(f32[64,10,1]{2,1,0:T(8,128)S(1)} %get-tuple-element.45), channel_id=1, source_target_pairs={{2,0},{4,2},{6,4},{0,6},{3,1},{5,3},{7,5},{1,7},{10,8},{12,10},{14... | collective-permute-start | bytes 7688 | tf_op jit(solution)/shard_map/ppermute | solution.py:22
  516.1 20.0 %collective-permute-start.66 = (f32[64,1,128]{2,1,0:T(1,128)S(1)}, f32[64,1,128]{2,1,0:T(1,128)S(1)}, u32[]{:S(2)}, u32[]{:S(2)}) collective-permute-start(f32[64,1,128]{2,1,0:T(1,128)S(1)} %get-tuple-element.76), channel_id=1, source_target_pairs={{8,0},{16,8},{24,16},{9,1},{17,9},{25,17},{10,2},{18,10},{26,18},{... | collective-permute-start | bytes 98312 | tf_op jit(solution)/shard_map/ppermute | solution.py:22
  517.4 18.7 %collective-permute-start.67 = (f32[64,1,128]{2,1,0:T(1,128)S(1)}, f32[64,1,128]{2,1,0:T(1,128)S(1)}, u32[]{:S(2)}, u32[]{:S(2)}) collective-permute-start(f32[64,1,128]{2,1,0:T(1,128)S(1)} %get-tuple-element.77), channel_id=1, source_target_pairs={{0,8},{8,16},{16,24},{1,9},{9,17},{17,25},{2,10},{10,18},{18,26},{... | collective-permute-start | bytes 98312 | tf_op jit(solution)/shard_map/ppermute | solution.py:21
  543.0 16.6 %collective-permute-start.70 = (f32[64,10,1]{2,1,0:T(8,128)S(1)}, f32[64,10,1]{2,1,0:T(8,128)S(1)}, u32[]{:S(2)}, u32[]{:S(2)}) collective-permute-start(f32[64,10,1]{2,1,0:T(8,128)S(1)} %get-tuple-element.42), channel_id=1, source_target_pairs={{0,2},{2,4},{4,6},{6,0},{1,3},{3,5},{5,7},{7,1},{8,10},{10,12},{12... | collective-permute-start | bytes 7688 | tf_op jit(solution)/shard_map/ppermute | solution.py:21
  544.5 19.6 %collective-permute-start.71 = (f32[64,10,1]{2,1,0:T(8,128)S(1)}, f32[64,10,1]{2,1,0:T(8,128)S(1)}, u32[]{:S(2)}, u32[]{:S(2)}) collective-permute-start(f32[64,10,1]{2,1,0:T(8,128)S(1)} %get-tuple-element.43), channel_id=1, source_target_pairs={{2,0},{4,2},{6,4},{0,6},{3,1},{5,3},{7,5},{1,7},{10,8},{12,10},{14... | collective-permute-start | bytes 7688 | tf_op jit(solution)/shard_map/ppermute | solution.py:22
  565.3 17.6 %collective-permute-start.74 = (f32[64,1,128]{2,1,0:T(1,128)S(1)}, f32[64,1,128]{2,1,0:T(1,128)S(1)}, u32[]{:S(2)}, u32[]{:S(2)}) collective-permute-start(f32[64,1,128]{2,1,0:T(1,128)S(1)} %get-tuple-element.70), channel_id=1, source_target_pairs={{8,0},{16,8},{24,16},{9,1},{17,9},{25,17},{10,2},{18,10},{26,18},{... | collective-permute-start | bytes 98312 | tf_op jit(solution)/shard_map/ppermute | solution.py:22
  566.6 16.3 %collective-permute-start.75 = (f32[64,1,128]{2,1,0:T(1,128)S(1)}, f32[64,1,128]{2,1,0:T(1,128)S(1)}, u32[]{:S(2)}, u32[]{:S(2)}) collective-permute-start(f32[64,1,128]{2,1,0:T(1,128)S(1)} %get-tuple-element.71), channel_id=1, source_target_pairs={{0,8},{8,16},{16,24},{1,9},{9,17},{17,25},{2,10},{10,18},{18,26},{... | collective-permute-start | bytes 98312 | tf_op jit(solution)/shard_map/ppermute | solution.py:21
  589.9 16.4 %collective-permute-start.78 = (f32[64,10,1]{2,1,0:T(8,128)S(1)}, f32[64,10,1]{2,1,0:T(8,128)S(1)}, u32[]{:S(2)}, u32[]{:S(2)}) collective-permute-start(f32[64,10,1]{2,1,0:T(8,128)S(1)} %get-tuple-element.40), channel_id=1, source_target_pairs={{0,2},{2,4},{4,6},{6,0},{1,3},{3,5},{5,7},{7,1},{8,10},{10,12},{12... | collective-permute-start | bytes 7688 | tf_op jit(solution)/shard_map/ppermute | solution.py:21
  591.3 20.5 %collective-permute-start.79 = (f32[64,10,1]{2,1,0:T(8,128)S(1)}, f32[64,10,1]{2,1,0:T(8,128)S(1)}, u32[]{:S(2)}, u32[]{:S(2)}) collective-permute-start(f32[64,10,1]{2,1,0:T(8,128)S(1)} %get-tuple-element.41), channel_id=1, source_target_pairs={{2,0},{4,2},{6,4},{0,6},{3,1},{5,3},{7,5},{1,7},{10,8},{12,10},{14... | collective-permute-start | bytes 7688 | tf_op jit(solution)/shard_map/ppermute | solution.py:22
  613.0 13.7 %collective-permute-start.80 = (f32[64,8,1]{2,1,0:T(8,128)S(1)}, f32[64,8,1]{2,1,0:T(8,128)S(1)}, u32[]{:S(2)}, u32[]{:S(2)}) collective-permute-start(f32[64,8,1]{2,1,0:T(8,128)S(1)} %get-tuple-element.62), channel_id=1, source_target_pairs={{2,0},{4,2},{6,4},{0,6},{3,1},{5,3},{7,5},{1,7},{10,8},{12,10},{14... | collective-permute-start | bytes 6152 | tf_op jit(solution)/shard_map/ppermute | solution.py:22
  634.2 78.7 %all-reduce.13.cloned.1.call-start = ((), (), s32[]{:S(2)}) async-start(), calls=%async_computation.6 | async-start | bytes 262144 | tf_op jit(solution)/shard_map/psum | solution.py:112
  668.1 70.0 %all-gather.5.cloned.1.call-start = ((), (), s32[]{:S(2)}) async-start(), calls=%async_computation.3 | async-start | bytes 1572864 | tf_op jit(solution)/shard_map/all_gather | solution.py:120
  (71 other events, 790.6 us)
Sparse Core Ops, SparseCore 0:
  277.3 34.0 all-reduce.10
  314.3 42.0 all-reduce.14
  634.3 33.7 all-reduce.8
  670.8 42.0 all-reduce.12
Sparse Core Ops, SparseCore 1:
  313.4 8.6 all-gather.2
  670.1 8.6 all-gather.4
